TPU v7x, 32 devices: a whole 2x2x4 slice. The times are simulated.
32 devices in a mesh: row: 4 (over y, x), col: 4 (over z), depth: 2 (over core).
Axes of the slice: x: 2, y: 2, z: 4, core: 2. Of those that a mesh axis runs over, the one named last changes fastest.
Arguments:
- orbitals: bfloat16 [2, 1024, 2, 4096], P(None, ('row', 'col'), 'depth'), may hold values from -20 to 20
- potential: float32 [2, 4096], P('depth'), may hold values from -6 to 6
Outputs:
- intersection: float32 [1024, 2, 1024], P(('row', 'depth'), None, 'col')
- applied: bfloat16 [2, 1024, 2, 4096], P(None, ('row', 'col'), 'depth')
All inputs are finite; a program needn't handle non-finite values.
Results may differ from a plain program's by a relative error of at most 0.001.
Values may be sent and summed in bfloat16 or wider, within the bound.
A program may use at most 128 MiB of HBM per device.

v0:
```python
import jax
import jax.numpy as jnp
from jax import lax
from jax.sharding import PartitionSpec as P

NX = 64


def with_halo(block, sides, width):
    for axis, dim in sides:
        count = lax.axis_size(axis)
        forward = [(i, i + 1) for i in range(count - 1)]
        forward.append((count - 1, 0))
        backward = [(target, source) for source, target in forward]
        low = lax.ppermute(
            lax.slice_in_dim(block, block.shape[dim] - width, None, axis=dim), axis, forward
        )
        high = lax.ppermute(lax.slice_in_dim(block, 0, width, axis=dim), axis, backward)
        block = jnp.concatenate([low, block, high], axis=dim)
    return block


def apply_operator(padded, potential):
    center = padded[:, :, 1:-1].astype(jnp.float32)
    below = padded[:, :, :-2].astype(jnp.float32)
    above = padded[:, :, 2:].astype(jnp.float32)
    flat_cells = center.shape[-1]
    xpos = jnp.arange(flat_cells) % NX
    yminus = jnp.roll(center, NX, axis=3)
    yplus = jnp.roll(center, -NX, axis=3)
    xminus = jnp.where(xpos == 0, jnp.roll(center, 1 - NX, axis=3), jnp.roll(center, 1, axis=3))
    xplus = jnp.where(
        xpos == NX - 1, jnp.roll(center, NX - 1, axis=3), jnp.roll(center, -1, axis=3)
    )
    lap = below + above + yminus + yplus + xminus + xplus - 6.0 * center
    return (-0.5 * lap + potential[None, None] * center).astype(jnp.bfloat16)


def contract(left, right):
    return lax.dot_general(
        left, right, (((1,), (1,)), ((), ())), preferred_element_type=jnp.float32
    )


def shards(orbitals, potential):
    parts, orbs, planes, cells = orbitals.shape
    flat = orbitals.reshape(parts, orbs, planes * cells)
    panel = lax.all_gather(flat, "col", axis=1, tiled=True)
    other = lax.all_gather(flat, "row", axis=1, tiled=True)
    padded = with_halo(orbitals, (("depth", 2),), 1)
    applied = apply_operator(padded, potential)
    dvol = 1.0 / (planes * lax.axis_size("depth") * cells)
    tile_cols = other.shape[1]
    real_rows = panel[0]
    imag_rows = panel[1]
    sreal = contract(real_rows, other[0]) + contract(imag_rows, other[1])
    simag = contract(real_rows, other[1]) - contract(imag_rows, other[0])
    summed = lax.psum_scatter(
        dvol * jnp.concatenate([sreal, simag], axis=1), "depth", scatter_dimension=0, tiled=True
    )
    intersection = summed.reshape(summed.shape[0], 2, tile_cols)
    intersection = lax.all_to_all(intersection, "col", split_axis=2, concat_axis=2, tiled=True)
    return (intersection, applied)


def solution(mesh):
    in_specs = (P(None, ("row", "col"), "depth", None), P("depth", None))
    out_specs = (P(("row", "depth"), None, "col"), P(None, ("row", "col"), "depth", None))
    return jax.shard_map(shards, mesh=mesh, in_specs=in_specs, out_specs=out_specs, check_vma=False)
```

profile of v0, /device:TPU:0, one launch (start us, length us, event | category | flops | bytes accessed | tf_op | source)
XLA Modules:
  0.0 186.1 jit_solution(16060242905263434024)
XLA Ops:
  7.2 0.0 all-gather.7.cloned.1.call-start
  7.2 0.7 all-gather.7.cloned.1.call-update
  7.9 0.0 all-gather.5.cloned.1.call-start
  8.0 0.7 all-gather.5.cloned.1.call-update
  8.7 0.0 reduce-scatter.2.cloned.1.call-start
  8.7 0.6 collective-permute-start
  9.3 0.1 collective-permute-start.1
  9.4 0.1 fusion.23
  9.4 0.7 fusion.20
  10.1 0.7 fusion.19
  10.8 1.8 fusion.21
  12.7 2.4 %fusion.22 = (f32[2,64,1,4032]{3,1,2,0:T(8,128)}, f32[2,64,1,4032]{3,1,2,0:T(8,128)}) fusion(bf16[2,64,1,4096]{3,1,2,0:T(8,128)(2,1)S(1)} %copy-done), kind=kLoop, calls=%fused_computation.32 | loop fusion | bytes 8257536 | tf_op jit(solution)/shard_map/jit(_roll_static)/slice | solution.py:30
  15.1 50.1 %all-gather.7.cloned.1.call-done = bf16[2,256,1,4096]{3,1,2,0:T(8,128)(2,1)} async-done(((bf16[2,64,1,4096]{3,1,2,0:T(8,128)(2,1)}), bf16[2,256,1,4096]{3,1,2,0:T(8,128)(2,1)}) %all-gather.7.cloned.1.call-update) | async-done | bytes 4194320 | tf_op jit(solution)/shard_map/all_gather | solution.py:49
  65.2 82.3 %all-gather.5.cloned.1.call-done = bf16[2,256,1,4096]{3,1,2,0:T(8,128)(2,1)} async-done(((bf16[2,64,1,4096]{3,1,2,0:T(8,128)(2,1)}), bf16[2,256,1,4096]{3,1,2,0:T(8,128)(2,1)}) %all-gather.5.cloned.1.call-update) | async-done | bytes 4194320 | tf_op jit(solution)/shard_map/all_gather | solution.py:48
  147.5 3.1 %fusion.7 = f32[256,256]{0,1:T(8,128)S(1)} fusion(bf16[2,256,1,4096]{3,1,2,0:T(8,128)(2,1)} %all-gather.5.cloned.1.call-done, bf16[2,256,1,4096]{3,1,2,0:T(8,128)(2,1)} %all-gather.7.cloned.1.call-done), kind=kOutput, calls=%fused_computation.14 | convolution fusion | flops 536870912 | bytes 4456448 | tf_op jit(solution)/shard_map/dot_general | solution.py:40
  150.6 0.3 copy-done.2
  150.9 2.5 %fusion.8 = f32[256,256]{0,1:T(8,128)S(1)} fusion(bf16[2,256,1,4096]{3,1,2,0:T(8,128)(2,1)} %all-gather.5.cloned.1.call-done, bf16[2,256,1,4096]{3,1,2,0:T(8,128)(2,1)S(1)} %copy-done.2), kind=kOutput, calls=%fused_computation.15 | convolution fusion | flops 536870912 | bytes 4456448 | tf_op jit(solution)/shard_map/dot_general | solution.py:40
  153.4 0.3 copy-done.3
  153.8 0.7 fusion.12
  154.5 0.7 fusion.11
  155.3 0.8 maximum_multiply_fusion
  156.1 0.0 reduce-scatter.2.cloned.1.call-update
  156.1 0.6 fusion.15
  156.7 2.4 %fusion.18 = (f32[2,64,1,4095]{3,1,2,0:T(8,128)}, f32[2,64,1,4095]{3,1,2,0:T(8,128)}) fusion(bf16[2,64,1,4096]{3,1,2,0:T(8,128)(2,1)S(1)} %copy-done), kind=kLoop, calls=%fused_computation.28 | loop fusion | bytes 8386560 | tf_op jit(solution)/shard_map/jit(_roll_static)/slice | solution.py:33
  159.1 3.5 %reduce-scatter.2.cloned.1.call-done = f32[128,512]{0,1:T(8,128)} async-done(((f32[256,512]{0,1:T(8,128)}), f32[128,512]{0,1:T(8,128)}) %reduce-scatter.2.cloned.1.call-update) | async-done | bytes 262160 | tf_op jit(solution)/shard_map/reduce_scatter | solution.py:58
  162.7 1.9 copy.7
  164.5 4.8 %all-to-all-start = ((f32[128,2,256]{0,1,2:T(2,128)}), f32[128,2,256]{0,1,2:T(2,128)S(1)}, u32[]{:S(2)}, u32[]{:S(2)}) async-start(f32[128,2,256]{0,1,2:T(2,128)} %copy.7), calls=%async_computation.1 | async-start | bytes 524288 | tf_op jit(solution)/shard_map/all_to_all | solution.py:62
  169.3 0.0 collective-permute-done
  169.3 0.0 collective-permute-done.1
  169.3 6.8 %fusion.6 = bf16[2,64,1,4096]{3,1,2,0:T(8,128)(2,1)} fusion(f32[2,64,1,4032]{3,1,2,0:T(8,128)} %get-tuple-element.15, f32[2,64,1,64]{3,1,2,0:T(8,128)S(1)} %get-tuple-element.17, f32[2,64,1,64]{3,1,2,0:T(8,128)S(1)} %get-tuple-element.16, f32[2,64,1,4032]{3,1,2,0:T(8,128)} %get-tuple-element.14, f32[2,64,1,63]{3,1,2,0:T(8,128)} %get-tuple-element.11, ...), kind=kLoop, calls=%fused_computation.11 | loop fusion | flops 11534336 | bytes 16801792 | tf_op jit(solution)/shard_map/convert_element_type | solution.py:36
  176.2 2.6 %all-to-all-done = f32[128,2,256]{0,1,2:T(2,128)S(1)} async-done(((f32[128,2,256]{0,1,2:T(2,128)}), f32[128,2,256]{0,1,2:T(2,128)S(1)}, u32[]{:S(2)}, u32[]{:S(2)}) %all-to-all-start) | async-done | bytes 262176 | tf_op jit(solution)/shard_map/all_to_all | solution.py:62
  178.7 0.8 copy.8
  (6 shorter events, 0.0 us)
Async XLA Ops:
  7.2 1.5 copy-start
  7.2 58.0 %all-gather.7.cloned.1.call-start = ((), (), s32[]{:S(2)}) async-start(), calls=%async_computation.4 | async-start | bytes 5242880 | tf_op jit(solution)/shard_map/all_gather | solution.py:49
  7.9 139.6 %all-gather.5.cloned.1.call-start = ((), (), s32[]{:S(2)}) async-start(), calls=%async_computation.3 | async-start | bytes 5242880 | tf_op jit(solution)/shard_map/all_gather | solution.py:48
  8.7 154.0 %reduce-scatter.2.cloned.1.call-start = ((), (), s32[]{:S(2)}) async-start(), calls=%async_computation.2 | async-start | bytes 786432 | tf_op jit(solution)/shard_map/reduce_scatter | solution.py:58
  8.7 160.6 %collective-permute-start = (bf16[2,64,1,4096]{3,1,2,0:T(8,128)(2,1)S(1)}, bf16[2,64,1,4096]{3,1,2,0:T(8,128)(2,1)}, u32[]{:S(2)}, u32[]{:S(2)}) collective-permute-start(bf16[2,64,1,4096]{3,1,2,0:T(8,128)(2,1)S(1)} %copy-done), channel_id=1, source_target_pairs={{0,1},{1,0},{2,3},{3,2},{4,5},{5,4},{6,7},{7,6},{8,9},{9,8},{10,11... | collective-permute-start | bytes 3145736 | tf_op jit(solution)/shard_map/ppermute | solution.py:15
  9.3 160.1 %collective-permute-start.1 = (bf16[2,64,1,4096]{3,1,2,0:T(8,128)(2,1)S(1)}, bf16[2,64,1,4096]{3,1,2,0:T(8,128)(2,1)}, u32[]{:S(2)}, u32[]{:S(2)}) collective-permute-start(bf16[2,64,1,4096]{3,1,2,0:T(8,128)(2,1)S(1)} %copy-done), channel_id=1, source_target_pairs={{1,0},{0,1},{3,2},{2,3},{5,4},{4,5},{7,6},{6,7},{9,8},{8,9},{11,10... | collective-permute-start | bytes 3145736 | tf_op jit(solution)/shard_map/ppermute | solution.py:18
  147.5 3.4 %copy-start.2 = (bf16[2,256,1,4096]{3,1,2,0:T(8,128)(2,1)S(1)}, bf16[2,256,1,4096]{3,1,2,0:T(8,128)(2,1)}, u32[]{:S(2)}) copy-start(bf16[2,256,1,4096]{3,1,2,0:T(8,128)(2,1)} %all-gather.7.cloned.1.call-done) | copy-start | bytes 12582916
  150.9 2.8 %copy-start.3 = (bf16[2,256,1,4096]{3,1,2,0:T(8,128)(2,1)S(1)}, bf16[2,256,1,4096]{3,1,2,0:T(8,128)(2,1)}, u32[]{:S(2)}) copy-start(bf16[2,256,1,4096]{3,1,2,0:T(8,128)(2,1)} %all-gather.5.cloned.1.call-done) | copy-start | bytes 12582916
  156.7 12.6 %copy-start.1 = (f32[1,4096]{1,0:T(1,128)S(1)}, f32[1,4096]{1,0:T(1,128)}, u32[]{:S(2)}) copy-start(f32[1,4096]{1,0:T(1,128)} %param.3) | copy-start | bytes 49156
  164.5 14.2 %all-to-all-start = ((f32[128,2,256]{0,1,2:T(2,128)}), f32[128,2,256]{0,1,2:T(2,128)S(1)}, u32[]{:S(2)}, u32[]{:S(2)}) async-start(f32[128,2,256]{0,1,2:T(2,128)} %copy.7), calls=%async_computation.1 | async-start | bytes 524288 | tf_op jit(solution)/shard_map/all_to_all | solution.py:62
Sparse Core Ops, SparseCore 0:
  9.8 55.2 all-gather.6
  66.7 80.7 all-gather.4
  156.2 6.3 reduce-scatter.1
where the time goes:
time: 186 us
  waiting for transfers between devices  140 us (75%)
  between operations  13.8 us (7%)
  local copies, waits for them, and re-layouts  11.5 us (6%)
  other arithmetic  8.25 us (4%)
  matrix products  7.07 us (4%)
  starting transfers between devices  5.54 us (3%)
    all_gather x1, waiting for transfers between devices, shards(): panel = lax.all_gather(flat, 'col', axis=1, tiled=True)  82.3 us
    all_gather x1, waiting for transfers between devices, shards(): other = lax.all_gather(flat, 'row', axis=1, tiled=True)  50.1 us
    dot_general x4, matrix products, contract(): lax.dot_general(left, right, (((1,), (1,)), ((), ())), preferred_element_...  7.07 us
    convert_element_type x1, other arithmetic, apply_operator(): return (-0.5 * lap + potential[None, None] * center).astype(jnp.bfloat16)  6.81 us
    all_to_all x1, starting transfers between devices, shards(): lax.all_to_all(intersection, 'col', split_axis=2, concat_axis=2, tiled=True)  4.79 us
  transfers between devices with their start and end apart: 6, of which 4 were waited for; matrix products, arithmetic and copies ran while one was open for 14% of the time, Pallas kernels for 0%

commit v1 on v0

--- a/solution.py
+++ b/solution.py
@@ -45,7 +45,9 @@
 def shards(orbitals, potential):
     parts, orbs, planes, cells = orbitals.shape
     flat = orbitals.reshape(parts, orbs, planes * cells)
-    panel = lax.all_gather(flat, "col", axis=1, tiled=True)
+    panel = jnp.concatenate(
+        lax.all_to_all(jnp.stack([flat] * lax.axis_size("col")), "col", 0, 0), axis=1
+    )
     other = lax.all_gather(flat, "row", axis=1, tiled=True)
     padded = with_halo(orbitals, (("depth", 2),), 1)
     applied = apply_operator(padded, potential)

time: 186 us -> 156 us (0.84)
  waiting for transfers between devices: 140 us -> 93.8 us
  local copies, waits for them, and re-layouts: 11.5 us -> 20.3 us
  starting transfers between devices: 5.54 us -> 11.9 us
    all_to_all x0 -> x1, waiting for transfers between devices: none -> 86.3 us  [shards(): lax.all_to_all(jnp.stack([flat] * lax.axis_size('col')), 'col', 0, 0)]
    all_gather x1 -> x0, waiting for transfers between devices: 82.3 us -> none  [shards(): panel = lax.all_gather(flat, 'col', axis=1, tiled=True)]
    all_gather x1, waiting for transfers between devices: 50.1 us -> 0.01 us  [shards(): other = lax.all_gather(flat, 'row', axis=1, tiled=True)]
    all_to_all x0 -> x1, starting transfers between devices: none -> 6.48 us  [shards(): lax.all_to_all(jnp.stack([flat] * lax.axis_size('col')), 'col', 0, 0)]
    slice x0 -> x1, local copies, waits for them, and re-layouts: none -> 4.75 us  [shards(): real_rows = panel[0]]
    another operation x0 -> x1, local copies, waits for them, and re-layouts: none -> 3.71 us  [shards(): jnp.stack([flat] * lax.axis_size('col'))]
  transfers between devices with their start and end apart: 6 -> 6, of which waited for: 4 -> 3; matrix products, arithmetic and copies ran while one was open for 14% -> 19% of each run, Pallas kernels for 0% -> 0%
where the time goes in v1:
time: 156 us
  waiting for transfers between devices  93.8 us (60%)
  local copies, waits for them, and re-layouts  20.3 us (13%)
  between operations  14.1 us (9%)
  starting transfers between devices  11.9 us (8%)
  other arithmetic  8.26 us (5%)
  matrix products  7.28 us (5%)
    all_to_all x1, waiting for transfers between devices, shards(): lax.all_to_all(jnp.stack([flat] * lax.axis_size('col')), 'col', 0, 0)  86.3 us
    dot_general x4, matrix products, contract(): lax.dot_general(left, right, (((1,), (1,)), ((), ())), preferred_element_...  7.28 us
    convert_element_type x1, other arithmetic, apply_operator(): return (-0.5 * lap + potential[None, None] * center).astype(jnp.bfloat16)  6.81 us
    all_to_all x1, starting transfers between devices, shards(): lax.all_to_all(jnp.stack([flat] * lax.axis_size('col')), 'col', 0, 0)  6.48 us
    all_to_all x1, starting transfers between devices, shards(): lax.all_to_all(intersection, 'col', split_axis=2, concat_axis=2, tiled=True)  4.82 us
    slice x1, local copies, waits for them, and re-layouts, shards(): real_rows = panel[0]  4.75 us
    reduce_scatter x1, waiting for transfers between devices, shards(): lax.psum_scatter(dvol * jnp.concatenate([sreal, simag], axis=1), 'depth',...  4.2 us
    another operation x1, local copies, waits for them, and re-layouts, shards(): jnp.stack([flat] * lax.axis_size('col'))  3.71 us
  transfers between devices with their start and end apart: 6, of which 3 were waited for; matrix products, arithmetic and copies ran while one was open for 19% of the time, Pallas kernels for 0%

profile of v1, /device:TPU:0, one launch (start us, length us, event | category | flops | bytes accessed | tf_op | source)
XLA Modules:
  0.0 155.6 jit_solution(7314318121682118000)
XLA Ops:
  7.2 3.7 %stack.3 = bf16[4,2,64,4096]{3,2,1,0:T(8,128)(2,1)} broadcast(bf16[2,64,4096]{2,1,0:T(8,128)(2,1)} %bitcast.22), dimensions={1,2,3} | broadcast | bytes 5242880 | tf_op jit(solution)/shard_map/stack | solution.py:49
  10.9 6.5 %all-to-all-start = ((bf16[4,2,64,4096]{3,2,1,0:T(8,128)(2,1)}), bf16[4,2,64,4096]{3,2,1,0:T(8,128)(2,1)}, u32[]{:S(2)}, u32[]{:S(2)}) async-start(bf16[4,2,64,4096]{3,2,1,0:T(8,128)(2,1)} %stack.3), calls=%async_computation | async-start | bytes 8388608 | tf_op jit(solution)/shard_map/all_to_all | solution.py:49
  17.4 0.0 all-gather.3.cloned.1.call-start
  17.4 0.7 all-gather.3.cloned.1.call-update
  18.1 0.0 reduce-scatter.2.cloned.1.call-start
  18.1 0.1 collective-permute-start
  18.2 0.5 collective-permute-start.1
  18.7 0.1 fusion.24
  18.8 0.7 fusion.21
  19.5 0.7 fusion.20
  20.2 1.8 %fusion.22 = (f32[2,64,1,4033]{3,1,2,0:T(8,128)S(1)}, f32[2,64,1,4033]{3,1,2,0:T(8,128)}) fusion(bf16[2,64,1,4096]{3,1,2,0:T(8,128)(2,1)S(1)} %copy-done), kind=kLoop, calls=%fused_computation.30 | loop fusion | bytes 8259584 | tf_op jit(solution)/shard_map/jit(_roll_static)/slice | solution.py:33
  22.0 2.4 %fusion.23 = (f32[2,64,1,4032]{3,1,2,0:T(8,128)}, f32[2,64,1,4032]{3,1,2,0:T(8,128)}) fusion(bf16[2,64,1,4096]{3,1,2,0:T(8,128)(2,1)S(1)} %copy-done), kind=kLoop, calls=%fused_computation.31 | loop fusion | bytes 8257536 | tf_op jit(solution)/shard_map/jit(_roll_static)/slice | solution.py:30
  24.4 86.3 %all-to-all-done = bf16[4,2,64,4096]{3,2,1,0:T(8,128)(2,1)} async-done(((bf16[4,2,64,4096]{3,2,1,0:T(8,128)(2,1)}), bf16[4,2,64,4096]{3,2,1,0:T(8,128)(2,1)}, u32[]{:S(2)}, u32[]{:S(2)}) %all-to-all-start) | async-done | bytes 4194336 | tf_op jit(solution)/shard_map/all_to_all | solution.py:49
  110.8 4.8 %fusion.18 = (bf16[1,4,64,4096]{3,2,0,1:T(8,128)(2,1)}, bf16[1,4,64,4096]{3,2,0,1:T(8,128)(2,1)}) fusion(bf16[2,4,64,4096]{3,2,0,1:T(8,128)(2,1)} %bitcast.1), kind=kLoop, calls=%fused_computation.26 | loop fusion | bytes 8388608 | tf_op jit(solution)/shard_map/slice | solution.py:56
  115.5 3.1 %fusion.7 = f32[256,256]{0,1:T(8,128)S(1)} fusion(bf16[256,4096]{1,0:T(8,128)(2,1)} %bitcast.23, bf16[2,256,1,4096]{3,1,2,0:T(8,128)(2,1)} %all-gather.3.cloned.1.call-done), kind=kOutput, calls=%fused_computation.12 | convolution fusion | flops 536870912 | bytes 4456448 | tf_op jit(solution)/shard_map/dot_general | solution.py:40
  118.7 2.7 %fusion.8 = f32[256,256]{0,1:T(8,128)S(1)} fusion(bf16[256,4096]{1,0:T(8,128)(2,1)S(1)} %bitcast.25, bf16[2,256,1,4096]{3,1,2,0:T(8,128)(2,1)} %all-gather.3.cloned.1.call-done), kind=kOutput, calls=%fused_computation.13 | convolution fusion | flops 536870912 | bytes 4456448 | tf_op jit(solution)/shard_map/dot_general | solution.py:40
  121.4 0.1 copy-done.4
  121.5 0.7 fusion.12
  122.2 0.8 copy-done.1
  123.1 0.7 fusion.11
  123.8 0.8 maximum_multiply_fusion
  124.6 0.0 reduce-scatter.2.cloned.1.call-update
  124.7 0.6 fusion.15
  125.3 2.4 %fusion.19 = (f32[2,64,1,4095]{3,1,2,0:T(8,128)}, f32[2,64,1,4095]{3,1,2,0:T(8,128)}) fusion(bf16[2,64,1,4096]{3,1,2,0:T(8,128)(2,1)S(1)} %copy-done), kind=kLoop, calls=%fused_computation.27 | loop fusion | bytes 8386560 | tf_op jit(solution)/shard_map/jit(_roll_static)/slice | solution.py:33
  127.7 4.2 %reduce-scatter.2.cloned.1.call-done = f32[128,512]{0,1:T(8,128)} async-done(((f32[256,512]{0,1:T(8,128)}), f32[128,512]{0,1:T(8,128)}) %reduce-scatter.2.cloned.1.call-update) | async-done | bytes 262160 | tf_op jit(solution)/shard_map/reduce_scatter | solution.py:60
  131.9 1.9 %copy.7 = f32[128,2,256]{0,1,2:T(2,128)} copy(f32[128,2,256]{0,2,1:T(8,128)} %bitcast.27) | data formatting | bytes 524288 | tf_op jit(solution)/shard_map/reshape | solution.py:63
  133.8 4.8 %all-to-all-start.1 = ((f32[128,2,256]{0,1,2:T(2,128)}), f32[128,2,256]{0,1,2:T(2,128)S(1)}, u32[]{:S(2)}, u32[]{:S(2)}) async-start(f32[128,2,256]{0,1,2:T(2,128)} %copy.7), calls=%async_computation.2 | async-start | bytes 524288 | tf_op jit(solution)/shard_map/all_to_all | solution.py:64
  138.6 0.0 collective-permute-done
  138.6 0.0 collective-permute-done.1
  138.6 6.8 %fusion.6 = bf16[2,64,1,4096]{3,1,2,0:T(8,128)(2,1)} fusion(f32[2,64,1,4032]{3,1,2,0:T(8,128)} %get-tuple-element.17, f32[2,64,1,64]{3,1,2,0:T(8,128)S(1)} %get-tuple-element.19, f32[2,64,1,64]{3,1,2,0:T(8,128)S(1)} %get-tuple-element.18, f32[2,64,1,4032]{3,1,2,0:T(8,128)} %get-tuple-element.16, f32[2,64,1,63]{3,1,2,0:T(8,128)} %get-tuple-element.13, ...), kind=kLoop, calls=%fused_computation.9 | loop fusion | flops 11534336 | bytes 16801792 | tf_op jit(solution)/shard_map/convert_element_type | solution.py:36
  145.4 2.5 %all-to-all-done.1 = f32[128,2,256]{0,1,2:T(2,128)S(1)} async-done(((f32[128,2,256]{0,1,2:T(2,128)}), f32[128,2,256]{0,1,2:T(2,128)S(1)}, u32[]{:S(2)}, u32[]{:S(2)}) %all-to-all-start.1) | async-done | bytes 262176 | tf_op jit(solution)/shard_map/all_to_all | solution.py:64
  148.0 0.8 copy.8
  (9 shorter events, 0.0 us)
Async XLA Ops:
  10.9 7.3 %copy-start = (bf16[2,64,1,4096]{3,1,2,0:T(8,128)(2,1)S(1)}, bf16[2,64,1,4096]{3,1,2,0:T(8,128)(2,1)}, u32[]{:S(2)}) copy-start(bf16[2,64,1,4096]{3,1,2,0:T(8,128)(2,1)} %param.2) | copy-start | bytes 3145732
  10.9 99.9 %all-to-all-start = ((bf16[4,2,64,4096]{3,2,1,0:T(8,128)(2,1)}), bf16[4,2,64,4096]{3,2,1,0:T(8,128)(2,1)}, u32[]{:S(2)}, u32[]{:S(2)}) async-start(bf16[4,2,64,4096]{3,2,1,0:T(8,128)(2,1)} %stack.3), calls=%async_computation | async-start | bytes 8388608 | tf_op jit(solution)/shard_map/all_to_all | solution.py:49
  17.4 98.2 %all-gather.3.cloned.1.call-start = ((), (), s32[]{:S(2)}) async-start(), calls=%async_computation.4 | async-start | bytes 5242880 | tf_op jit(solution)/shard_map/all_gather | solution.py:51
  18.1 113.8 %reduce-scatter.2.cloned.1.call-start = ((), (), s32[]{:S(2)}) async-start(), calls=%async_computation.3 | async-start | bytes 786432 | tf_op jit(solution)/shard_map/reduce_scatter | solution.py:60
  18.1 120.5 %collective-permute-start = (bf16[2,64,1,4096]{3,1,2,0:T(8,128)(2,1)S(1)}, bf16[2,64,1,4096]{3,1,2,0:T(8,128)(2,1)}, u32[]{:S(2)}, u32[]{:S(2)}) collective-permute-start(bf16[2,64,1,4096]{3,1,2,0:T(8,128)(2,1)S(1)} %copy-done), channel_id=1, source_target_pairs={{0,1},{1,0},{2,3},{3,2},{4,5},{5,4},{6,7},{7,6},{8,9},{9,8},{10,11... | collective-permute-start | bytes 3145736 | tf_op jit(solution)/shard_map/ppermute | solution.py:15
  18.2 120.4 %collective-permute-start.1 = (bf16[2,64,1,4096]{3,1,2,0:T(8,128)(2,1)S(1)}, bf16[2,64,1,4096]{3,1,2,0:T(8,128)(2,1)}, u32[]{:S(2)}, u32[]{:S(2)}) collective-permute-start(bf16[2,64,1,4096]{3,1,2,0:T(8,128)(2,1)S(1)} %copy-done), channel_id=1, source_target_pairs={{1,0},{0,1},{3,2},{2,3},{5,4},{4,5},{7,6},{6,7},{9,8},{8,9},{11,10... | collective-permute-start | bytes 3145736 | tf_op jit(solution)/shard_map/ppermute | solution.py:18
  115.5 3.1 %copy-start.2 = (bf16[1,4,64,4096]{3,2,0,1:T(8,128)(2,1)S(1)}, bf16[1,4,64,4096]{3,2,0,1:T(8,128)(2,1)}, u32[]{:S(2)}) copy-start(bf16[1,4,64,4096]{3,2,0,1:T(8,128)(2,1)} %get-tuple-element.6) | copy-start | bytes 6291460
  118.7 2.8 %copy-start.4 = (bf16[2,256,1,4096]{3,1,2,0:T(8,128)(2,1)S(1)}, bf16[2,256,1,4096]{3,1,2,0:T(8,128)(2,1)}, u32[]{:S(2)}) copy-start(bf16[2,256,1,4096]{3,1,2,0:T(8,128)(2,1)} %all-gather.3.cloned.1.call-done) | copy-start | bytes 12582916
  121.5 1.6 %copy-start.1 = (bf16[1,4,64,4096]{3,2,0,1:T(8,128)(2,1)S(1)}, bf16[1,4,64,4096]{3,2,0,1:T(8,128)(2,1)}, u32[]{:S(2)}) copy-start(bf16[1,4,64,4096]{3,2,0,1:T(8,128)(2,1)} %get-tuple-element.7) | copy-start | bytes 6291460
  125.3 13.3 %copy-start.3 = (f32[1,4096]{1,0:T(1,128)S(1)}, f32[1,4096]{1,0:T(1,128)}, u32[]{:S(2)}) copy-start(f32[1,4096]{1,0:T(1,128)} %param.3) | copy-start | bytes 49156
  133.8 14.2 %all-to-all-start.1 = ((f32[128,2,256]{0,1,2:T(2,128)}), f32[128,2,256]{0,1,2:T(2,128)S(1)}, u32[]{:S(2)}, u32[]{:S(2)}) async-start(f32[128,2,256]{0,1,2:T(2,128)} %copy.7), calls=%async_computation.2 | async-start | bytes 524288 | tf_op jit(solution)/shard_map/all_to_all | solution.py:64
Sparse Core Ops, SparseCore 0:
  20.0 54.0 all-gather.2
  124.8 7.0 reduce-scatter.1
